TPU v7x, 8 devices: a whole 2x2x1 slice. The times are simulated.
8 devices in a mesh: fsdp: 4 (over z, y, x), tp: 2 (over core).
Axes of the slice: x: 2, y: 2, z: 1, core: 2. Of those that a mesh axis runs over, the one named last changes fastest.
Arguments:
- x: bfloat16 [32768, 5120], P(('fsdp', 'tp'))
- gamma: float32 [5120], replicated
- w1: bfloat16 [5120, 13824], P('fsdp', 'tp')
- w2: bfloat16 [13824, 5120], P('tp', 'fsdp')
Outputs:
- output: bfloat16 [32768, 5120], P(('fsdp', 'tp'))
All inputs are finite; a program needn't handle non-finite values.
Results may differ from a plain program's by a relative error of at most 0.001.
Values are sent between devices in bfloat16 or wider.
A program may use at most 1 GiB of HBM per device.

v0:
```python
import jax
import jax.numpy as jnp
from jax import lax
from jax.sharding import PartitionSpec as P

EPS = 1e-6


def _norm(x, gamma):
    xf = x.astype(jnp.float32)
    mu = jnp.mean(xf, axis=-1, keepdims=True)
    var = jnp.mean(jnp.square(xf - mu), axis=-1, keepdims=True)
    return xf, ((xf - mu) * lax.rsqrt(var + EPS) * gamma).astype(jnp.bfloat16)


def solution(mesh):
    def body(x, gamma, w1, w2):
        w1f = lax.all_gather(w1, "fsdp", axis=0, tiled=True)
        w2f = lax.all_gather(w2, "fsdp", axis=1, tiled=True)
        xf, xn = _norm(x, gamma)
        xg = lax.all_gather(xn, "tp", axis=0, tiled=True)
        h = jax.nn.gelu(jnp.dot(xg, w1f, preferred_element_type=jnp.float32), approximate=True).astype(jnp.bfloat16)
        yp = jnp.dot(h, w2f, preferred_element_type=jnp.float32)
        y = lax.psum_scatter(yp, "tp", scatter_dimension=0, tiled=True)
        return (xf + y).astype(jnp.bfloat16)

    return jax.shard_map(
        body,
        mesh=mesh,
        in_specs=(P(("fsdp", "tp"), None), P(None), P("fsdp", "tp"), P("tp", "fsdp")),
        out_specs=P(("fsdp", "tp"), None),
        check_vma=False,
    )
```

profile of v0, /device:TPU:0, one launch (start us, length us, event | category | flops | bytes accessed | tf_op | source)
XLA Modules:
  0.0 2275.4 jit_solution(17653682275067536475)
XLA Ops:
  6.5 0.0 copy-start
  6.5 0.0 all-gather.4.cloned.1.call-start
  6.5 13.8 convert_reduce_fusion
  20.3 15.7 fusion.12
  36.0 0.0 copy-done
  36.0 28.3 %fusion.14 = bf16[4096,5120]{1,0:T(8,128)(2,1)} fusion(bf16[4096,5120]{1,0:T(8,128)(2,1)} %param.4, f32[5120]{0:T(1024)S(1)} %copy-done, f32[4096]{0:T(1024)S(1)} %add_rsqrt_fusion, f32[4096]{0:T(1024)S(1)} %broadcast_multiply_fusion), kind=kLoop, calls=%fused_computation.17 | loop fusion | flops 104857600 | bytes 83939328 | tf_op jit(solution)/shard_map/convert_element_type | solution.py:13
  64.3 0.0 all-gather.4.cloned.1.call-update
  64.3 0.0 all-gather.6.cloned.1.call-start
  64.4 0.7 all-gather.6.cloned.1.call-update
  65.1 0.0 all-gather.8.cloned.1.call-start
  65.1 0.7 all-gather.8.cloned.1.call-update
  65.8 0.0 reduce-scatter.5.cloned.1.call-start
  65.9 112.7 %all-gather.4.cloned.1.call-done = bf16[8192,5120]{1,0:T(8,128)(2,1)} async-done(((bf16[4096,5120]{1,0:T(8,128)(2,1)}), bf16[8192,5120]{1,0:T(8,128)(2,1)}) %all-gather.4.cloned.1.call-update) | async-done | bytes 83886096 | tf_op jit(solution)/shard_map/all_gather | solution.py:21
  178.6 605.5 %all-gather.6.cloned.1.call-done = bf16[5120,6912]{1,0:T(8,128)(2,1)} async-done(((bf16[1280,6912]{1,0:T(8,128)(2,1)}), bf16[5120,6912]{1,0:T(8,128)(2,1)}) %all-gather.6.cloned.1.call-update) | async-done | bytes 70778896 | tf_op jit(solution)/shard_map/all_gather | solution.py:18
  784.1 604.2 %fusion.20 = f32[8192,6912]{1,0:T(8,128)} fusion(bf16[8192,5120]{1,0:T(8,128)(2,1)} %all-gather.4.cloned.1.call-done, bf16[5120,6912]{1,0:T(8,128)(2,1)} %all-gather.6.cloned.1.call-done), kind=kOutput, calls=%fused_computation.25 | convolution fusion | flops 579820584960 | bytes 381157376 | tf_op jit(solution)/shard_map/dot_general | solution.py:22
  1388.3 0.2 all-gather.8.cloned.1.call-done
  1388.5 662.5 %fusion.8 = f32[8192,5120]{1,0:T(8,128)} fusion(bf16[6912,5120]{1,0:T(8,128)(2,1)} %all-gather.8.cloned.1.call-done, f32[8192,6912]{1,0:T(8,128)} %fusion.20), kind=kOutput, calls=%fused_computation.12 | convolution fusion | flops 580330192896 | bytes 465043456 | tf_op jit(solution)/shard_map/dot_general | solution.py:23
  2051.0 0.0 reduce-scatter.5.cloned.1.call-update
  2051.0 164.7 %reduce-scatter.5.cloned.1.call-done = f32[4096,5120]{1,0:T(8,128)} async-done(((f32[8192,5120]{1,0:T(8,128)}), f32[4096,5120]{1,0:T(8,128)}) %reduce-scatter.5.cloned.1.call-update) | async-done | bytes 83886096
  2215.7 53.2 %fusion.15 = bf16[4096,5120]{1,0:T(8,128)(2,1)} fusion(f32[4096,5120]{1,0:T(8,128)} %reduce-scatter.5.cloned.1.call-done, bf16[4096,5120]{1,0:T(8,128)(2,1)} %param.4), kind=kLoop, calls=%fused_computation.18 | loop fusion | flops 62914560 | bytes 167772160 | tf_op jit(solution)/shard_map/convert_element_type | solution.py:25
  (2 shorter events, 0.0 us)
Async XLA Ops:
  6.5 29.5 %copy-start = (f32[5120]{0:T(1024)S(1)}, f32[5120]{0:T(1024)}, u32[]{:S(2)}) copy-start(f32[5120]{0:T(1024)} %param.5) | copy-start | bytes 61444
  6.5 172.0 %all-gather.4.cloned.1.call-start = ((), (), s32[]{:S(2)}) async-start(), calls=%async_computation.1 | async-start | bytes 125829120 | tf_op jit(solution)/shard_map/all_gather | solution.py:21
  64.3 719.8 %all-gather.6.cloned.1.call-start = ((), (), s32[]{:S(2)}) async-start(), calls=%async_computation.2 | async-start | bytes 88473600 | tf_op jit(solution)/shard_map/all_gather | solution.py:18
  65.1 1323.4 %all-gather.8.cloned.1.call-start = ((), (), s32[]{:S(2)}) async-start(), calls=%async_computation.3 | async-start | bytes 88473600 | tf_op jit(solution)/shard_map/all_gather | solution.py:19
  65.8 2149.9 %reduce-scatter.5.cloned.1.call-start = ((), (), s32[]{:S(2)}) async-start(), calls=%async_computation.4 | async-start | bytes 251658240
Sparse Core Ops, SparseCore 0:
  64.4 114.0 all-gather.3
  180.4 603.6 all-gather.5
  785.9 602.4 all-gather.7
  2051.1 164.4 reduce-scatter.4
where the time goes:
time: 2280 us
  matrix products  1270 us (56%)
  waiting for transfers between devices  884 us (39%)
  other arithmetic  111 us (5%)
    dot_general x1, matrix products, body(): yp = jnp.dot(h, w2f, preferred_element_type=jnp.float32)  663 us
    all_gather x1, waiting for transfers between devices, body(): w1f = lax.all_gather(w1, 'fsdp', axis=0, tiled=True)  606 us
    dot_general x1, matrix products, body(): jnp.dot(xg, w1f, preferred_element_type=jnp.float32)  604 us
    unnamed x5, waiting for transfers between devices  166 us
    all_gather x1, waiting for transfers between devices, body(): xg = lax.all_gather(xn, 'tp', axis=0, tiled=True)  113 us
    convert_element_type x1, other arithmetic, body(): return (xf + y).astype(jnp.bfloat16)  53.2 us
  transfers between devices with their start and end apart: 4, of which 4 were waited for; matrix products, arithmetic and copies ran while one was open for 27% of the time, Pallas kernels for 0%

commit v1 on v0

v1 whole, which is shorter than its diff:
```python
import jax
import jax.numpy as jnp
from jax import lax
from jax.experimental import pallas as pl
from jax.experimental.pallas import tpu as pltpu
from jax.sharding import PartitionSpec as P

EPS = 1e-6
MESH = pl.DeviceIdType.MESH
BF16 = jnp.bfloat16
F32 = jnp.float32

ROWS, D, F = 4096, 5120, 13824
DS, FS = D // 4, F // 2
CH = 256
NCH = FS // CH
LB, LS = 256, 32
MB = 1024
NM = ROWS // MB
HB = 256
NH = ROWS // HB
MD, ND = 512, 256
GS = 64
TC = 256
NT = DS // TC
GT = 3
NG = -(-4 * NT // GT)
FH = FS // 2


def _mo(v, m):
    return pl.multiple_of(v, m)


def _kernel(x_ref, g_ref, w1_ref, w2_ref, y_ref, w1g, w2g, h_ref, ss, r1, r2, lx, lw, lh, l2w, l2x, l2y):
    a = lax.axis_index("fsdp")
    b = lax.axis_index("tp")
    ay, ax = a // 2, a % 2
    ob = 1 - b

    def nb(ry, rx):
        return ((ay + ry) % 2) * 2 + (ax + rx) % 2

    aX, aY, aD = nb(0, 1), nb(1, 0), nb(1, 1)
    devX, devY, devS = (aX, b), (aY, b), (a, ob)

    bar = pltpu.get_barrier_semaphore()
    for dev in (devX, devY, devS):
        pl.semaphore_signal(bar, inc=1, device_id=dev, device_id_type=MESH)
    pl.semaphore_wait(bar, 3)

    def send(src, dst, s, r, dev):
        pltpu.make_async_remote_copy(
            src_ref=src, dst_ref=dst, send_sem=s, recv_sem=r, device_id=dev, device_id_type=MESH
        ).start()

    def recv(dst, s, r, dev):
        pltpu.make_async_remote_copy(
            src_ref=dst, dst_ref=dst, send_sem=s, recv_sem=r, device_id=dev, device_id_type=MESH
        ).wait_recv()

    def w1_own(c):
        return w1_ref.at[:, pl.ds(_mo(c * CH, CH), CH)]

    def direct(c):
        send(w1_own(c), w1g.at[b, a, c], ss.at[0], r1.at[0, c], devX)
        send(w1_own(c), w1g.at[b, a, c], ss.at[1], r1.at[1, c], devY)
        send(w1_own(c), w1g.at[b, a, c], ss.at[4], r1.at[4, c], devS)

    def on_direct(c):
        recv(w1g.at[b, aX, c], ss.at[0], r1.at[0, c], devX)
        recv(w1g.at[b, aY, c], ss.at[1], r1.at[1, c], devY)
        top, bot = pl.ds(0, DS // 2), pl.ds(DS // 2, DS // 2)
        send(w1g.at[b, aY, c, top], w1g.at[b, aY, c, top], ss.at[2], r1.at[2, c], devX)
        send(w1g.at[b, aX, c, bot], w1g.at[b, aX, c, bot], ss.at[3], r1.at[3, c], devY)
        send(w1g.at[b, aX, c], w1g.at[b, aX, c], ss.at[5], r1.at[5, c], devS)
        send(w1g.at[b, aY, c], w1g.at[b, aY, c], ss.at[6], r1.at[6, c], devS)

    def on_relay(c):
        top, bot = pl.ds(0, DS // 2), pl.ds(DS // 2, DS // 2)
        recv(w1g.at[b, aD, c, top], ss.at[2], r1.at[2, c], devX)
        recv(w1g.at[b, aD, c, bot], ss.at[3], r1.at[3, c], devY)
        send(w1g.at[b, aD, c], w1g.at[b, aD, c], ss.at[7], r1.at[7, c], devS)

    def on_sib(c):
        for k, s in ((4, a), (5, aX), (6, aY), (7, aD)):
            recv(w1g.at[ob, s, c], ss.at[k], r1.at[k, c], devS)

    def cols(t):
        return pl.ds(_mo(t * TC, TC), TC)

    def w2_at(bb, s, t, rows=None):
        return w2g.at[bb, s, slice(None) if rows is None else rows, cols(t)]

    def w2_direct(t):
        send(w2_ref.at[:, cols(t)], w2_at(b, a, t), ss.at[8], r2.at[0, t], devX)
        send(w2_ref.at[:, cols(t)], w2_at(b, a, t), ss.at[9], r2.at[1, t], devY)

    def w2_sib_own(t):
        send(w2_ref.at[:, cols(t)], w2_at(b, a, t), ss.at[12], r2.at[4, t], devS)

    def w2_got_direct(t):
        for k, s, dev in ((0, aX, devX), (1, aY, devY)):
            recv(w2_at(b, s, t), ss.at[8 + k], r2.at[k, t], dev)
            send(w2_at(b, s, t), w2_at(b, s, t), ss.at[13 + k], r2.at[5 + k, t], devS)

    def w2_relay(t):
        for k, s, dev in ((0, aY, devX), (1, aX, devY)):
            v = w2_at(b, s, t, pl.ds(k * FH, FH))
            send(v, v, ss.at[10 + k], r2.at[2 + k, t], dev)

    def w2_got_relay(t):
        for k, dev in ((0, devX), (1, devY)):
            recv(w2_at(b, aD, t, pl.ds(k * FH, FH)), ss.at[10 + k], r2.at[2 + k, t], dev)
        send(w2_at(b, aD, t), w2_at(b, aD, t), ss.at[15], r2.at[7, t], devS)

    def w2_got_sib(rel, t):
        recv(w2_at(ob, (a, aX, aY, aD)[rel], t), ss.at[12 + rel], r2.at[4 + rel, t], devS)

    def upto(f, lo, hi):
        lax.fori_loop(lo, hi, lambda c, _: (f(c), 0)[1], 0)

    def lead(j):
        return jnp.minimum(NCH - 1, j + 1 + j // 14)

    def phase1(xn, gm, wb, acc0, acc1, hb):
        def x_load(i):
            rows = pl.ds(_mo(i * LB, LB), LB)
            return pltpu.make_async_copy(x_ref.at[rows, :], xn.at[rows, :], lx.at[i])

        direct(0)
        gcp = pltpu.make_async_copy(g_ref, gm, lx.at[ROWS // LB])
        gcp.start()

        @pl.loop(0, ROWS // LB)
        def _(i):
            x_load(i).start()

        gcp.wait()

        @pl.loop(0, ROWS // LB)
        def _(i):
            x_load(i).wait()

            @pl.when(i == 7)
            def _():
                on_direct(0)
                direct(1)
                direct(2)

            @pl.loop(0, LB // LS)
            def _(t):
                rows = pl.ds(_mo(i * LB + t * LS, LS), LS)
                xf = xn[rows, :].astype(F32)
                mu = jnp.mean(xf, axis=-1, keepdims=True)
                xc = xf - mu
                var = jnp.mean(jnp.square(xc), axis=-1, keepdims=True)
                xn[rows, :] = (xc * lax.rsqrt(var + EPS) * gm[0:1, :]).astype(BF16)

        def w_load(c, s):
            own, sib = pl.ds(0, CH), pl.ds(CH, CH)

            def rows(v):
                return pl.ds(_mo(v * DS, DS), DS)

            def cp(src, dst):
                pltpu.make_async_copy(src, dst, lw.at[s]).start()

            cp(w1_own(c), wb.at[s, rows(a), own])
            for v in (aX, aY, aD):
                cp(w1g.at[b, v, c], wb.at[s, rows(v), own])
            for v in (a, aX, aY, aD):
                cp(w1g.at[ob, v, c], wb.at[s, rows(v), sib])

        def h_store(j, m, s, half):
            off = (b if half == 0 else ob) * FS + j * CH
            return pltpu.make_async_copy(
                hb.at[s, half],
                h_ref.at[pl.ds(_mo(m * MB, MB), MB), pl.ds(_mo(off, CH), CH)],
                lh.at[s, half],
            )

        on_relay(0)
        on_sib(0)
        w_load(0, 0)
        acc1[...] = jnp.zeros_like(acc1)

        accs = (acc0, acc1)

        def finish(u):
            for r in range(0, MB, GS):
                for half in (0, 1):
                    v = accs[u][r : r + GS, half * CH : (half + 1) * CH]
                    hb[u, half, r : r + GS] = jax.nn.gelu(v, approximate=True).astype(BF16)

        def store(t, u):
            for half in (0, 1):
                h_store(t // NM, t % NM, u, half).start()

        def stored(u):
            for half in (0, 1):
                h_store(0, 0, u, half).wait()

        def events(j, m, s):
            more = j + 1 < NCH
            if m == 0:

                def take(c):
                    on_direct(c)

                    @pl.when(c + 2 < NCH)
                    def _():
                        direct(c + 2)

                upto(take, jnp.where(j == 0, 1, lead(j - 1) + 1), lead(j) + 1)
            if m == 1:

                @pl.when((j >= 14) & (j < 14 + NT))
                def _():
                    w2_sib_own(j - 14)

                @pl.when(j == NCH - 3)
                def _():
                    w2_direct(0)
                    w2_direct(1)

            if m == 2:

                @pl.when(more)
                def _():
                    on_relay(j + 1)

            if m == 3:

                @pl.when(more)
                def _():
                    on_sib(j + 1)
                    w_load(j + 1, 1 - s)

        @pl.loop(0, NCH)
        def _(j):
            s = j % 2
            pltpu.make_async_copy(wb.at[1 - s], wb.at[s], lw.at[s]).wait()

            @pl.loop(0, NM // 2)
            def _(m2):
                for u in (0, 1):
                    t = j * NM + m2 * 2 + u

                    for em in (u, u + 2):

                        @pl.when(m2 == em // 2)
                        def _(em=em):
                            events(j, em, s)

                    @pl.when(t > 2)
                    def _(u=u):
                        stored(1 - u)

                    finish(1 - u)
                    for r in range(0, MB, MD):
                        rows = pl.ds(_mo((m2 * 2 + u) * MB + r, MD), MD)
                        for c in range(0, 2 * CH, ND):
                            accs[u][r : r + MD, c : c + ND] = jnp.dot(
                                xn[rows, :], wb[s, :, c : c + ND], preferred_element_type=F32
                            )

                    @pl.when(t > 0)
                    def _(t=t, u=u):
                        store(t - 1, 1 - u)

        stored(1)
        finish(1)
        store(NCH * NM - 1, 1)
        for u in (0, 1):
            stored(u)

    pl.run_scoped(
        phase1,
        pltpu.VMEM((ROWS, D), BF16),
        pltpu.VMEM((8, D), F32),
        pltpu.VMEM((2, D, 2 * CH), BF16),
        pltpu.VMEM((MB, 2 * CH), F32),
        pltpu.VMEM((MB, 2 * CH), F32),
        pltpu.VMEM((2, 2, MB, CH), BF16),
    )

    def phase2(w0, w1, hb, xb, yb):
        sets = (w0, w1)

        def shard_of(n):
            mid = n - NT
            rx = jnp.where(n < NT, 0, jnp.where(n < 3 * NT, 1 - mid % 2, 1))
            ry = jnp.where(n < NT, 0, jnp.where(n < 3 * NT, mid % 2, 1))
            t = jnp.where(n < NT, n, jnp.where(n < 3 * NT, mid // 2, n - 3 * NT))
            return nb(ry, rx), t

        def w_load(n):
            g, k = n // GT, n % GT
            dst, sem = sets[g % 2], l2w.at[g % 2]
            tc = pl.ds(k * TC, TC)
            mid = n - NT
            if n < NT:
                src, t, rel = w2_ref.at[:, cols(n)], n, 0
            elif n < 3 * NT:
                t, rel = mid // 2, 1 + mid % 2
                src = w2_at(b, (aX, aY)[mid % 2], t)
            else:
                t, rel = n - 3 * NT, 3
                src = w2_at(b, aD, t)
            w2_got_sib(rel, t)
            pltpu.make_async_copy(src, dst.at[pl.ds(_mo(b * FS, FS), FS), tc], sem).start()
            osrc = w2_at(ob, (a, aX, aY, aD)[rel], t)
            pltpu.make_async_copy(osrc, dst.at[pl.ds(_mo(ob * FS, FS), FS), tc], sem).start()

        def w_wait(p, nt):
            v = sets[p].at[:, pl.ds(0, nt * TC)]
            pltpu.make_async_copy(v, v, l2w.at[p]).wait()

        def h_load(i, s):
            return pltpu.make_async_copy(h_ref.at[pl.ds(_mo(i * HB, HB), HB), :], hb.at[s], lx.at[s])

        def tiles(g, i, s, x, nt):
            for k in range(nt):
                owner, t = shard_of(g * GT + k)
                there = pl.ds(_mo(i * HB, HB), HB), pl.ds(_mo(owner * DS + t * TC, TC), TC)
                here = s, slice(None), pl.ds(k * TC, TC)
                if x:
                    yield pltpu.make_async_copy(x_ref.at[there], xb.at[here], l2x.at[s, k])
                else:
                    yield pltpu.make_async_copy(yb.at[here], y_ref.at[there], l2y.at[s, k])

        def each(g, i, s, x, act, last=False):
            for k, c in enumerate(tiles(g, i, s, x, GT - last)):
                getattr(c, act)()

        ev = {
            (0, 0): lambda: (w2_direct(2), w_load(3), w_load(4)),
            (0, 4): lambda: w2_got_direct(0),
            (0, 6): lambda: w_load(5),
            (1, 0): lambda: (w2_got_direct(1), w2_direct(3), w_load(6)),
            (1, 3): lambda: (w_load(7), w_load(8)),
            (2, 0): lambda: (w2_got_direct(2), w2_direct(4)),
            (2, 3): lambda: (w_load(9), w_load(10)),
            (2, 11): lambda: (w2_got_direct(3), w2_relay(0), w2_relay(1)),
            (2, 13): lambda: w_load(11),
            (3, 0): lambda: w_load(12),
            (3, 8): lambda: (w2_got_direct(4), w2_relay(2), w2_relay(3), w2_relay(4)),
            (3, 10): lambda: (w_load(13), w_load(14)),
            (4, 1): lambda: w2_got_relay(0),
            (4, 3): lambda: w_load(15),
            (4, 6): lambda: w2_got_relay(1),
            (4, 8): lambda: w_load(16),
            (4, 12): lambda: w2_got_relay(2),
            (4, 14): lambda: w_load(17),
            (5, 2): lambda: w2_got_relay(3),
            (5, 5): lambda: w_load(18),
            (5, 9): lambda: w2_got_relay(4),
            (5, 12): lambda: w_load(19),
        }

        h_load(0, 0).start()
        each(0, 0, 0, True, "start")
        for n in range(GT):
            w_load(n)

        def group(g, p, last):
            nt = 4 * NT - GT * (NG - 1) if last else GT
            w_wait(p, nt)

            @pl.loop(0, NH)
            def _(i):
                s = i % 2
                if not last:
                    h_load((i + 1) % NH, 1 - s).start()

                    @pl.when(i + 1 < NH)
                    def _():
                        each(g, i + 1, 1 - s, True, "start")

                    @pl.when((i + 1 == NH) & (g < NG - 2))
                    def _():
                        each(g + 1, 0, 0, True, "start")

                    @pl.when((i + 1 == NH) & (g == NG - 2))
                    def _():
                        each(NG - 1, 0, 0, True, "start", True)

                    for (eg, ei), f in ev.items():
                        if eg % 2 == p:

                            @pl.when((g == eg) & (i == ei))
                            def _(f=f):
                                f()
                else:

                    @pl.when(i + 1 < NH)
                    def _():
                        h_load(i + 1, 1 - s).start()
                        each(g, i + 1, 1 - s, True, "start", True)

                h_load(i, s).wait()
                each(g, i, s, True, "wait", last)
                if last:

                    @pl.when(i < 2)
                    def _():
                        each(NG - 2, i, s, False, "wait")

                    @pl.when(i > 1)
                    def _():
                        each(g, i, s, False, "wait", True)
                else:

                    @pl.when((g > 0) | (i > 1))
                    def _():
                        each(g, i, s, False, "wait")

                n = nt * TC
                d = jnp.dot(hb[s], sets[p][:, :n], preferred_element_type=F32)
                yb[s, :, :n] = (xb[s, :, :n].astype(F32) + d).astype(BF16)
                each(g, i, s, False, "start", last)

        @pl.loop(0, (NG - 1) // 2)
        def _(q):
            for p in (0, 1):
                group(2 * q + p, p, False)

        group(NG - 1, 0, True)
        for i in (0, 1):
            each(NG - 1, i, i, False, "wait", True)

    pl.run_scoped(
        phase2,
        pltpu.VMEM((F, GT * TC), BF16),
        pltpu.VMEM((F, GT * TC), BF16),
        pltpu.VMEM((2, HB, F), BF16),
        pltpu.VMEM((2, HB, GT * TC), BF16),
        pltpu.VMEM((2, HB, GT * TC), BF16),
    )

    def drain(ref, k):
        pltpu.make_async_copy(ref, ref, ss.at[k]).wait()

    for k in (0, 1, 4, 5, 6, 7):
        drain(w1_ref, k)
    for k in (2, 3):
        drain(w1_ref.at[pl.ds(0, DS // 2), :], k)
    for k in (8, 9, 12, 13, 14, 15):
        drain(w2_ref, k)
    for k in (10, 11):
        drain(w2_ref.at[pl.ds(0, FH), :], k)


def solution(mesh):
    any_spec = pl.BlockSpec(memory_space=pl.ANY)

    def body(x, gamma, w1, w2):
        y, _, _, _ = pl.pallas_call(
            _kernel,
            out_shape=(
                jax.ShapeDtypeStruct((ROWS, D), BF16),
                jax.ShapeDtypeStruct((2, 4, NCH, DS, CH), BF16),
                jax.ShapeDtypeStruct((2, 4, FS, DS), BF16),
                jax.ShapeDtypeStruct((ROWS, F), BF16),
            ),
            in_specs=[any_spec] * 4,
            out_specs=(any_spec,) * 4,
            scratch_shapes=[
                pltpu.SemaphoreType.DMA((16,)),
                pltpu.SemaphoreType.DMA((8, NCH)),
                pltpu.SemaphoreType.DMA((8, NT)),
                pltpu.SemaphoreType.DMA((ROWS // LB + 1,)),
                pltpu.SemaphoreType.DMA((2,)),
                pltpu.SemaphoreType.DMA((2, 2)),
                pltpu.SemaphoreType.DMA((2,)),
                pltpu.SemaphoreType.DMA((2, GT)),
                pltpu.SemaphoreType.DMA((2, GT)),
            ],
            compiler_params=pltpu.CompilerParams(
                collective_id=0, has_side_effects=True, vmem_limit_bytes=67043328
            ),
            cost_estimate=pl.CostEstimate(
                flops=4 * ROWS * D * F, bytes_accessed=2 * 10**9, transcendentals=ROWS * F
            ),
            name="mlp",
        )(x, jnp.broadcast_to(gamma, (8, D)), w1, w2)
        return y

    return jax.shard_map(
        body,
        mesh=mesh,
        in_specs=(P(("fsdp", "tp"), None), P(None), P("fsdp", "tp"), P("tp", "fsdp")),
        out_specs=P(("fsdp", "tp"), None),
        check_vma=False,
    )
```

time: 2280 us -> 1350 us (0.59)
  Pallas kernels: 0 us -> 1320 us
  matrix products: 1270 us -> 0 us
  waiting for transfers between devices: 884 us -> 0 us
  other arithmetic: 111 us -> 0 us
  local copies, waits for them, and re-layouts: 0.01 us -> 29.6 us
    pallas_call x0 -> x1, Pallas kernels: none -> 1320 us  [body(): pl.pallas_call(_kernel, out_shape=(jax.ShapeDtypeStruct((ROWS, D), BF16),...]
    dot_general x2 -> x0, matrix products: 1270 us -> none  [the longest x1 663 us: body(): yp = jnp.dot(h, w2f, preferred_element_type=jnp.float32)]
    all_gather x3 -> x0, waiting for transfers between devices: 718 us -> none  [the longest x1 606 us: body(): w1f = lax.all_gather(w1, 'fsdp', axis=0, tiled=True)]
    unnamed x5 -> x0, waiting for transfers between devices: 166 us -> none
    convert_element_type x2 -> x0, other arithmetic: 81.4 us -> none  [the longest x1 53.2 us: body(): return (xf + y).astype(jnp.bfloat16)]
    reduce_sum x2 -> x0, other arithmetic: 29.5 us -> none  [the longest x1 15.7 us: _norm(): var = jnp.mean(jnp.square(xf - mu), axis=-1, keepdims=True)]
    unnamed x2 -> x1, local copies, waits for them, and re-layouts: 0.01 us -> 28.2 us
  transfers between devices with their start and end apart: 4 -> 0, of which waited for: 4 -> 0; matrix products, arithmetic and copies ran while one was open for 27% -> 0% of each run, Pallas kernels for 0% -> 0%
where the time goes in v1:
time: 1350 us
  Pallas kernels  1320 us (98%)
  local copies, waits for them, and re-layouts  29.6 us (2%)
    pallas_call x1, Pallas kernels, body(): pl.pallas_call(_kernel, out_shape=(jax.ShapeDtypeStruct((ROWS, D), BF16),...  1320 us
    unnamed x1, local copies, waits for them, and re-layouts  28.2 us

profile of v1, /device:TPU:0, one launch (start us, length us, event | category | flops | bytes accessed | tf_op | source)
XLA Modules:
  0.0 1351.8 jit_solution(8850560856641063161)
XLA Ops:
  0.0 1.4 broadcast_in_dim.3.g_ref
  1.4 1322.2 %mlp.1 = (bf16[4096,5120]{1,0:T(8,128)(2,1)}, bf16[2,4,27,1280,256]{4,3,2,1,0:T(8,128)(2,1)}, bf16[2,4,6912,1280]{3,2,1,0:T(8,128)(2,1)}, bf16[4096,13824]{1,0:T(8,128)(2,1)}) custom-call(bf16[4096,5120]{1,0:T(8,128)(2,1)} %x_ref.1, f32[8,5120]{1,0:T(8,128)} %broadcast_in_dim.3.g_ref, bf16[1280,6912]{1,0:T(8,128)(2,1)} %w1_ref.1, bf16[6912,1280]{1,0:T(8,128)(2,1)} %w2_ref.1), custom_call_target="tpu_custom_call" | custom-call | flops 1159641169920 | bytes 2000000000 | tf_op jit(solution)/shard_map/mlp/pallas_call | solution.py:459
  1323.6 28.2 %copy.6 = bf16[4096,5120]{1,0:T(8,128)(2,1)} copy(bf16[4096,5120]{1,0:T(8,128)(2,1)} %get-tuple-element.6) | data formatting | bytes 83886080

commit v2 on v1

--- a/solution.py
+++ b/solution.py
@@ -128,6 +128,21 @@
             rows = pl.ds(_mo(i * LB, LB), LB)
             return pltpu.make_async_copy(x_ref.at[rows, :], xn.at[rows, :], lx.at[i])
 
+        def w_load(c, s):
+            own, sib = pl.ds(0, CH), pl.ds(CH, CH)
+
+            def rows(v):
+                return pl.ds(_mo(v * DS, DS), DS)
+
+            def cp(src, dst):
+                pltpu.make_async_copy(src, dst, lw.at[s]).start()
+
+            cp(w1_own(c), wb.at[s, rows(a), own])
+            for v in (aX, aY, aD):
+                cp(w1g.at[b, v, c], wb.at[s, rows(v), own])
+            for v in (a, aX, aY, aD):
+                cp(w1g.at[ob, v, c], wb.at[s, rows(v), sib])
+
         direct(0)
         gcp = pltpu.make_async_copy(g_ref, gm, lx.at[ROWS // LB])
         gcp.start()
@@ -147,6 +162,15 @@
                 on_direct(0)
                 direct(1)
                 direct(2)
+
+            @pl.when(i == 12)
+            def _():
+                on_relay(0)
+
+            @pl.when(i == 14)
+            def _():
+                on_sib(0)
+                w_load(0, 0)
 
             @pl.loop(0, LB // LS)
             def _(t):
@@ -157,21 +181,6 @@
                 var = jnp.mean(jnp.square(xc), axis=-1, keepdims=True)
                 xn[rows, :] = (xc * lax.rsqrt(var + EPS) * gm[0:1, :]).astype(BF16)
 
-        def w_load(c, s):
-            own, sib = pl.ds(0, CH), pl.ds(CH, CH)
-
-            def rows(v):
-                return pl.ds(_mo(v * DS, DS), DS)
-
-            def cp(src, dst):
-                pltpu.make_async_copy(src, dst, lw.at[s]).start()
-
-            cp(w1_own(c), wb.at[s, rows(a), own])
-            for v in (aX, aY, aD):
-                cp(w1g.at[b, v, c], wb.at[s, rows(v), own])
-            for v in (a, aX, aY, aD):
-                cp(w1g.at[ob, v, c], wb.at[s, rows(v), sib])
-
         def h_store(j, m, s, half):
             off = (b if half == 0 else ob) * FS + j * CH
             return pltpu.make_async_copy(
@@ -180,9 +189,6 @@
                 lh.at[s, half],
             )
 
-        on_relay(0)
-        on_sib(0)
-        w_load(0, 0)
         acc1[...] = jnp.zeros_like(acc1)
 
         accs = (acc0, acc1)
@@ -331,7 +337,7 @@
                     yield pltpu.make_async_copy(yb.at[here], y_ref.at[there], l2y.at[s, k])
 
         def each(g, i, s, x, act, last=False):
-            for k, c in enumerate(tiles(g, i, s, x, GT - last)):
+            for c in tiles(g, i, s, x, GT - last):
                 getattr(c, act)()
 
         ev = {
@@ -386,12 +392,15 @@
                     def _():
                         each(NG - 1, 0, 0, True, "start", True)
 
-                    for (eg, ei), f in ev.items():
-                        if eg % 2 == p:
-
-                            @pl.when((g == eg) & (i == ei))
-                            def _(f=f):
-                                f()
+                    for eg in range(p, NG - 1, 2):
+
+                        @pl.when(g == eg)
+                        def _(eg=eg):
+                            for (fg, ei), f in ev.items():
+                                if fg == eg:
+                                    @pl.when(i == ei)
+                                    def _(f=f):
+                                        f()
                 else:
 
                     @pl.when(i + 1 < NH)

time: 1350 us -> 1340 us (level)
  no operation moved by 1% of the time
where the time goes in v2:
time: 1340 us
  Pallas kernels  1310 us (98%)
  local copies, waits for them, and re-layouts  29.6 us (2%)
    pallas_call x1, Pallas kernels, body(): pl.pallas_call(_kernel, out_shape=(jax.ShapeDtypeStruct((ROWS, D), BF16),...  1310 us
    unnamed x1, local copies, waits for them, and re-layouts  28.2 us

profile of v2, /device:TPU:0, one launch (start us, length us, event | category | flops | bytes accessed | tf_op | source)
XLA Modules:
  0.0 1342.5 jit_solution(8464015628288946525)
XLA Ops:
  0.0 1.4 broadcast_in_dim.3.g_ref
  1.4 1312.9 %mlp.1 = (bf16[4096,5120]{1,0:T(8,128)(2,1)}, bf16[2,4,27,1280,256]{4,3,2,1,0:T(8,128)(2,1)}, bf16[2,4,6912,1280]{3,2,1,0:T(8,128)(2,1)}, bf16[4096,13824]{1,0:T(8,128)(2,1)}) custom-call(bf16[4096,5120]{1,0:T(8,128)(2,1)} %x_ref.1, f32[8,5120]{1,0:T(8,128)} %broadcast_in_dim.3.g_ref, bf16[1280,6912]{1,0:T(8,128)(2,1)} %w1_ref.1, bf16[6912,1280]{1,0:T(8,128)(2,1)} %w2_ref.1), custom_call_target="tpu_custom_call" | custom-call | flops 1159641169920 | bytes 2000000000 | tf_op jit(solution)/shard_map/mlp/pallas_call | solution.py:468
  1314.3 28.2 %copy.6 = bf16[4096,5120]{1,0:T(8,128)(2,1)} copy(bf16[4096,5120]{1,0:T(8,128)(2,1)} %get-tuple-element.6) | data formatting | bytes 83886080
